TPU v7x, 32 devices: a whole 2x2x4 slice. The times are simulated.
32 devices in a mesh: blk: 8 (over z, y), head: 4 (over x, core).
Axes of the slice: x: 2, y: 2, z: 4, core: 2. Of those that a mesh axis runs over, the one named last changes fastest.
Arguments:
- queries: bfloat16 [4096, 1024], P('blk', 'head'), may hold values from -170 to 170
- key_rows: bfloat16 [4096, 1024], P('blk', 'head'), may hold values from -9 to 9
- values: bfloat16 [4096, 1024], P('blk', 'head'), may hold values from -48 to 48
- text_keys: bfloat16 [308, 1024], P(None, 'head'), may hold values from -9 to 9
- text_values: bfloat16 [308, 1024], P(None, 'head'), may hold values from -48 to 48
- block_image: int32 [32], replicated, may hold values from 0 to 1, as said below
- gate_image: float32 [2, 1536], replicated, may hold values from 0.5 to 2
- residual: bfloat16 [4096, 1536], P(('blk', 'head')), may hold values from -6 to 6
- w_out: bfloat16 [1024, 1536], P('head'), may hold values from -0.1875 to 0.1875
Outputs:
- stream_out: bfloat16 [4096, 1536], P(('blk', 'head'))
Inputs may be any that keep to these rules, and one draw needn't show every extreme that they name: `block_image`: each image number 0 to 1 names 8 to 24 of the entries, some image exactly 24 and some exactly 8; the blocks of an image lie anywhere in the array.
All inputs are finite; a program needn't handle non-finite values.
Results may differ from a plain program's by a relative error of at most 0.014.
Values may be sent and summed in bfloat16 or wider, within the bound.
A program may use at most 64 MiB of HBM per device.

v0:
```python
import functools

import jax
import jax.numpy as jnp
from jax import lax
from jax.experimental import pallas as pl
from jax.experimental.pallas import tpu as pltpu
from jax.sharding import PartitionSpec as P

HD = 64
TEXT = 154
BS = 128
NEG = -1e30
LANES = 128
QTILE = 512
KEYS = 1024
MESH = pl.DeviceIdType.MESH
F32 = jnp.float32
BF16 = jnp.bfloat16


def partner(z, i):
    out, bit = z, 1
    while bit <= i:
        if i & bit:
            out = out + bit - 2 * bit * ((out // bit) % 2)
        bit *= 2
    return out


def kernel(
    n, nh, q_ref, k_ref, v_ref, tk_ref, tv_ref, img_ref, gate_ref, res_ref, w_ref, out_ref,
    qs, kvs, qr, kvr, traw, qaug, kaug, kval, taug, tval, best, accum, osend, orecv, mixed, wfull, resv,
    q_send, q_recv, kv_send, kv_recv, wx_send, ws_send, w_recv, o_send, o_recv, l_sem,
):
    tok, cols = q_ref.shape
    heads = cols // HD
    groups = n // heads
    half = tok // 2
    images = gate_ref.shape[0]
    wrows = w_ref.shape[0]
    td = res_ref.shape[0]
    texts = tk_ref.shape[0]
    per = tok // BS
    b = lax.axis_index("blk")
    j = lax.axis_index("head")
    z, r = b % heads, b // heads
    side, core = j // 2, j % 2

    barrier = pltpu.get_barrier_semaphore()
    count = 0
    for i in range(heads):
        for k in range(nh):
            if i or k:
                to = (r * heads + partner(z, i), lax.rem(j + k, nh))
                pl.semaphore_signal(barrier, inc=1, device_id=to, device_id_type=MESH)
                count += 1
    for k in range(1, groups):
        for i in range(heads):
            to = (lax.rem(r + k, groups) * heads + partner(z, i), j)
            pl.semaphore_signal(barrier, inc=1, device_id=to, device_id_type=MESH)
            count += 1

    w_here = pltpu.make_async_copy(w_ref, wfull.at[pl.ds(pl.multiple_of(j * wrows, wrows), wrows)], l_sem.at[0])
    w_here.start()
    res_here = pltpu.make_async_copy(res_ref, resv, l_sem.at[1])
    res_here.start()

    for h in range(heads):
        c = slice(h * HD, (h + 1) * HD)
        q = q_ref[:, c] * BF16(HD ** -0.5)
        qs[h] = jnp.concatenate([q[:half], q[half:]], axis=1)
        kvs[h] = jnp.concatenate([k_ref[:, c], v_ref[:, c]], axis=1)

    pl.semaphore_wait(barrier, count)

    def remote(src, dst, ss, rs, to):
        return pltpu.make_async_remote_copy(
            src_ref=src, dst_ref=dst, send_sem=ss, recv_sem=rs, device_id=to, device_id_type=MESH
        )

    sent = []

    def go(copy):
        copy.start()
        sent.append(copy)

    def wrow(owner):
        return wfull.at[pl.ds(pl.multiple_of(owner * wrows, wrows), wrows)]

    def send_kv(i, k):
        other = partner(z, i)
        pos = (groups - k) % groups * heads + i
        go(remote(kvs.at[other], kvr.at[pos], kv_send.at[pos], kv_recv.at[pos],
                  (lax.rem(r + k, groups) * heads + other, j)))

    for i in range(1, heads):
        other = partner(z, i)
        go(remote(qs.at[other], qr.at[i], q_send.at[i], q_recv.at[i], (r * heads + other, j)))
    for i in range(1, heads):
        send_kv(i, 0)
    for i in range(heads):
        for k in range(1, groups):
            send_kv(i, k)
    sib = side * 2 + 1 - core
    go(remote(w_ref, wrow(j), ws_send.at[0], w_recv.at[j], (b, sib)))
    for k in range(1, nh // 2):
        to = lax.rem(side + k, nh // 2) * 2 + core
        go(remote(w_ref, wrow(j), wx_send.at[k], w_recv.at[j], (b, to)))

    lane = lax.broadcasted_iota(jnp.int32, (16, LANES), 1)
    low_f = (lane < HD).astype(F32)
    low = low_f.astype(BF16)[:1]
    high = (1.0 - low_f).astype(BF16)[:1]

    def onehot(image):
        return jnp.where(lane == HD + image, 1.0, 0.0).astype(BF16)[:1]

    def others(image):
        return jnp.where((lane < HD) | (lane == HD + image), 0.0, NEG).astype(BF16)[:1]

    traw[...] = jnp.zeros_like(traw)
    for h in range(heads):
        c = slice(h * HD, (h + 1) * HD)

        @pl.when(z == h)
        def _():
            traw[pl.ds(0, texts), :] = jnp.concatenate([tk_ref[:, c], tv_ref[:, c]], axis=1).astype(F32)

    trow = lax.broadcasted_iota(jnp.int32, traw.shape, 0)
    tlane = lax.broadcasted_iota(jnp.int32, traw.shape, 1)
    timg = jnp.zeros_like(trow)
    for i in range(1, images + 1):
        timg += (trow >= i * TEXT).astype(jnp.int32)
    raw = traw[...]
    taug[...] = jnp.where(tlane < HD, raw, jnp.where(tlane == HD + timg, 1.0, 0.0)).astype(BF16)
    tval[...] = jnp.where(tlane < HD, 1.0, raw).astype(BF16)

    def load_q(i):
        src = qs.at[z] if i == 0 else qr.at[i]
        first = (r * heads + partner(z, i)) * per
        for p in range(per):
            at = (p * BS) % half
            x = src[pl.ds(at, BS), :]
            if p * BS >= half:
                x = pltpu.roll(x.astype(F32), HD, 1).astype(BF16)
            qaug[pl.ds(i * tok + p * BS, BS), :] = x * low + others(img_ref[first + p])

    def load_kv(pos):
        first = (lax.rem(r + pos // heads, groups) * heads + partner(z, pos % heads)) * per
        for p in range(per):
            x = kvr[pos, pl.ds(p * BS, BS), :]
            rows = pl.ds(pos * tok + p * BS, BS)
            kaug[rows, :] = x * low + onehot(img_ref[first + p])
            kval[rows, :] = x * high + low

    def absorb(keys, vals, start, count, fresh):
        def body(t, carry):
            rows = pl.ds(pl.multiple_of(start + t * QTILE, QTILE), QTILE)
            s = lax.dot_general(qaug[rows, :], keys(), (((1,), (1,)), ((), ())), preferred_element_type=F32)
            top = jnp.broadcast_to(jnp.max(s, axis=1, keepdims=True), (QTILE, LANES))
            if not fresh:
                old = best[rows, :]
                top = jnp.maximum(old, top)
            wide = jnp.concatenate([top] * (s.shape[1] // LANES), axis=1)
            p = jnp.exp(s - wide).astype(BF16)
            add = jnp.dot(p, vals(), preferred_element_type=F32)
            if fresh:
                accum[rows, :] = add
            else:
                accum[rows, :] = accum[rows, :] * jnp.exp(old - top) + add
            best[rows, :] = top
            return carry

        lax.fori_loop(0, count // QTILE, body, 0, unroll=1)

    kvr[0] = kvs[z]
    for i in range(heads):
        if i:
            remote(qs.at[0], qr.at[i], q_send.at[i], q_recv.at[i], (b, sib)).wait_recv()
        load_q(i)
        absorb(lambda: taug[...], lambda: tval[...], i * tok, tok, True)

    join = max(1, min(heads, KEYS // tok))

    def arrive(pos):
        remote(kvs.at[0], kvr.at[pos], kv_send.at[0], kv_recv.at[pos], (b, sib)).wait_recv()

    def relay_w():
        for k in range(1, nh // 2):
            owner = lax.rem(side + nh // 2 - k, nh // 2) * 2 + core
            remote(w_ref, wrow(owner), ws_send.at[k], w_recv.at[owner], (b, sib)).wait_recv()
            go(remote(wrow(owner), wrow(owner), ws_send.at[k], w_recv.at[owner], (b, sib)))

    def finish(i):
        low2 = lax.broadcasted_iota(jnp.int32, (td // 2, LANES), 1) < HD
        to_blk = r * heads + partner(z, i)
        slot = j * heads + z
        for k in range(nh):
            dest = lax.rem(j + k, nh)
            base = pl.multiple_of(i * tok + dest * td, td)
            one = accum[pl.ds(base, td // 2), :]
            two = accum[pl.ds(base + td // 2, td // 2), :]
            one_r, two_r = pltpu.roll(one, HD, 1), pltpu.roll(two, HD, 1)
            y = (jnp.where(low2, one_r, two) / jnp.where(low2, one, two_r)).astype(BF16)
            if i == 0 and k == 0:
                orecv[slot] = y
            else:
                osend[i * nh + k] = y
                go(remote(osend.at[i * nh + k], orecv.at[slot], o_send.at[i * nh + k], o_recv.at[slot],
                          (to_blk, dest)))

    for g in range(0, n, join):
        for pos in range(g, g + join):
            if pos:
                arrive(pos)
            load_kv(pos)
        at = pl.ds(g * tok, join * tok)
        args = (lambda: kaug[at, :], lambda: kval[at, :])
        if g + join == n:
            relay_w()
            for s in reversed(range(heads)):
                absorb(*args, s * tok, tok, False)
                finish(s)
        else:
            absorb(*args, 0, heads * tok, False)

    w_here.wait()
    res_here.wait()
    for k in range(nh // 2):
        owner = lax.rem(side + nh // 2 - k, nh // 2) * 2 + 1 - core
        remote(w_ref, wrow(owner), ws_send.at[k], w_recv.at[owner], (b, sib)).wait_recv()
    for i in range(heads):
        for k in range(nh):
            if i or k:
                slot = lax.rem(j + k, nh) * heads + partner(z, i)
                remote(osend.at[0], orecv.at[slot], o_send.at[0], o_recv.at[slot], (b, sib)).wait_recv()
    low2 = lax.broadcasted_iota(jnp.int32, (td // 2, LANES), 1) < HD
    for p in range(heads * nh // 2):
        even, odd = orecv[2 * p].astype(F32), orecv[2 * p + 1].astype(F32)
        c = pl.ds(p * LANES, LANES)
        mixed[pl.ds(0, td // 2), c] = jnp.where(low2, even, pltpu.roll(odd, HD, 1)).astype(BF16)
        mixed[pl.ds(td // 2, td // 2), c] = jnp.where(low2, pltpu.roll(even, HD, 1), odd).astype(BF16)

    unit = min(td, BS)
    width = 256
    for t in range(out_ref.shape[1] // width):
        c = pl.ds(t * width, width)
        y = jnp.dot(mixed[...], wfull[:, c], preferred_element_type=F32)
        for u in range(td // unit):
            image = img_ref[(b * tok + j * td + u * unit) // BS]
            gate = jnp.zeros((1, width), F32)
            for m in range(images):
                gate = jnp.where(image == m, gate_ref[pl.ds(m, 1), c], gate)
            rows = pl.ds(u * unit, unit)
            part = y[u * unit:(u + 1) * unit]
            out_ref[rows, c] = (resv[rows, c].astype(F32) + gate * part).astype(BF16)

    for copy in sent:
        copy.wait_send()


def solution(mesh):
    n, nh = mesh.shape["blk"], mesh.shape["head"]

    def on_device(q, k, v, tk, tv, block_image, gate, res, w):
        tok, cols = q.shape
        heads = cols // HD
        groups = n // heads
        td = res.shape[0]
        rows = heads * tok
        upad = -(-tk.shape[0] // LANES) * LANES
        vm = pl.BlockSpec(memory_space=pltpu.VMEM)
        anyw = pl.BlockSpec(memory_space=pl.ANY)
        dma = pltpu.SemaphoreType.DMA
        return pl.pallas_call(
            functools.partial(kernel, n, nh),
            out_shape=jax.ShapeDtypeStruct(res.shape, BF16),
            in_specs=[vm, vm, vm, vm, vm, pl.BlockSpec(memory_space=pltpu.SMEM), vm, anyw, anyw],
            out_specs=vm,
            scratch_shapes=[
                pltpu.VMEM((heads, tok // 2, LANES), BF16),
                pltpu.VMEM((heads, tok, LANES), BF16),
                pltpu.VMEM((heads, tok // 2, LANES), BF16),
                pltpu.VMEM((n, tok, LANES), BF16),
                pltpu.VMEM((upad, LANES), F32),
                pltpu.VMEM((rows, LANES), BF16),
                pltpu.VMEM((n * tok, LANES), BF16),
                pltpu.VMEM((n * tok, LANES), BF16),
                pltpu.VMEM((upad, LANES), BF16),
                pltpu.VMEM((upad, LANES), BF16),
                pltpu.VMEM((rows, LANES), F32),
                pltpu.VMEM((rows, LANES), F32),
                pltpu.VMEM((heads * nh, td // 2, LANES), BF16),
                pltpu.VMEM((heads * nh, td // 2, LANES), BF16),
                pltpu.VMEM((td, heads * nh * HD), BF16),
                pltpu.VMEM((w.shape[0] * nh, w.shape[1]), BF16),
                pltpu.VMEM(res.shape, BF16),
                dma((heads,)), dma((heads,)), dma((n,)), dma((n,)),
                dma((nh,)), dma((nh,)), dma((nh,)), dma((heads * nh,)), dma((heads * nh,)), dma((2,)),
            ],
            compiler_params=pltpu.CompilerParams(
                collective_id=0, has_side_effects=True, vmem_limit_bytes=60 * 1024 * 1024
            ),
        )(q, k, v, tk, tv, block_image, gate, res, w)

    placed = (
        P("blk", "head"), P("blk", "head"), P("blk", "head"), P(None, "head"), P(None, "head"),
        P(), P(), P(("blk", "head"), None), P("head", None),
    )
    return jax.shard_map(
        on_device, mesh=mesh, in_specs=placed, out_specs=P(("blk", "head"), None), check_vma=False
    )
```

profile of v0, /device:TPU:0, one launch (start us, length us, event | category | flops | bytes accessed | tf_op | source)
XLA Modules:
  0.0 41.7 jit_solution(14882909399995310047)
XLA Ops:
  0.0 39.9 %shard_map.91 = bf16[128,1536]{1,0:T(8,128)(2,1)} custom-call(bf16[512,256]{1,0:T(8,128)(2,1)} %q_ref.1, bf16[512,256]{1,0:T(8,128)(2,1)} %k_ref.1, bf16[512,256]{1,0:T(8,128)(2,1)} %v_ref.1, bf16[308,256]{1,0:T(8,128)(2,1)} %tk_ref.1, bf16[308,256]{1,0:T(8,128)(2,1)} %tv_ref.1, s32[32]{0:T(128)} %img_ref.1, f32[2,1536]{1,0:T(2,128)} %gate_ref.1, ...), custom_call_target="tpu_custom_call" | custom-call | tf_op jit(solution)/shard_map/pallas_call | solution.py:276
  39.9 1.8 %copy.11 = bf16[128,1536]{1,0:T(8,128)(2,1)} copy(bf16[128,1536]{1,0:T(8,128)(2,1)} %shard_map.91) | data formatting | bytes 786432
where the time goes:
time: 41.8 us; the launch traced here: 41.7 us
  Pallas kernels  39.9 us (95%)
  local copies, waits for them, and re-layouts  1.77 us (4%)
    pallas_call x1, Pallas kernels, on_device(): pl.pallas_call(functools.partial(kernel, n, nh), out_shape=jax.ShapeDtype...  39.9 us
    unnamed x1, local copies, waits for them, and re-layouts  1.77 us

commit v1 on v0

--- a/solution.py
+++ b/solution.py
@@ -260,6 +260,303 @@
         copy.wait_send()
 
 
+QROWS = 128
+VROWS = 80
+
+
+def split_kernel(
+    n, nh, q_ref, k_ref, v_ref, tk_ref, tv_ref, img_ref, gate_ref, res_ref, w_ref, out_ref,
+    qin, kin, vin, tkin, tvin, qt, vt, ks, kr, qa, kaug, va, traw, sb, mb, osend, lsend, orecv, lrecv,
+    mixed, wfull, resv,
+    q_send, q_recv, k_send, k_recv, v_send, v_recv, wx_send, ws_send, w_recv, o_send, o_recv, e_send, e_recv, l_sem,
+):
+    tok, cols = q_ref.shape
+    heads = cols // HD
+    groups = n // heads
+    half = tok // 2
+    images = gate_ref.shape[0]
+    wrows = w_ref.shape[0]
+    td = res_ref.shape[0]
+    texts = tk_ref.shape[0]
+    share = -(-texts // groups)
+    keys = heads * tok
+    allk = kaug.shape[0]
+    tpad = allk - keys
+    per = tok // BS
+    b = lax.axis_index("blk")
+    j = lax.axis_index("head")
+    z, r = b % heads, b // heads
+    side, core = j // 2, j % 2
+
+    barrier = pltpu.get_barrier_semaphore()
+    count = 0
+    for k in range(groups):
+        for i in range(heads):
+            if i or k:
+                to = (lax.rem(r + k, groups) * heads + partner(z, i), j)
+                pl.semaphore_signal(barrier, inc=1, device_id=to, device_id_type=MESH)
+                count += 1
+    for k in range(1, nh):
+        pl.semaphore_signal(barrier, inc=1, device_id=(b, lax.rem(j + k, nh)), device_id_type=MESH)
+        count += 1
+
+    local = []
+    for s, (src, dst) in enumerate(
+        ((v_ref, vin), (q_ref, qin), (k_ref, kin), (tk_ref, tkin), (tv_ref, tvin),
+         (w_ref, wfull.at[pl.ds(pl.multiple_of(j * wrows, wrows), wrows)]), (res_ref, resv))
+    ):
+        copy = pltpu.make_async_copy(src, dst, l_sem.at[s])
+        copy.start()
+        local.append(copy)
+
+    def remote(src, dst, ss, rs, to):
+        return pltpu.make_async_remote_copy(
+            src_ref=src, dst_ref=dst, send_sem=ss, recv_sem=rs, device_id=to, device_id_type=MESH
+        )
+
+    sent = []
+
+    def go(copy):
+        copy.start()
+        sent.append(copy)
+
+    local[0].wait()
+    vt[...] = jnp.transpose(vin[...])
+    local[2].wait()
+    for h in range(heads):
+        c = slice(h * HD, (h + 1) * HD)
+        kh = kin[:, c]
+        ks[h] = jnp.concatenate([kh[:half], kh[half:]], axis=1)
+    local[1].wait()
+    qt[...] = jnp.transpose(qin[...]) * BF16(HD ** -0.5)
+
+    pl.semaphore_wait(barrier, count)
+
+    def hrows(h):
+        return pl.ds(pl.multiple_of(h * HD, HD), HD)
+
+    for i in range(1, heads):
+        other = partner(z, i)
+        to = (r * heads + other, j)
+        go(remote(ks.at[other], kr.at[i], k_send.at[i], k_recv.at[i], to))
+        go(remote(vt.at[hrows(other)], va.at[pl.ds(0, HD), pl.ds(i * tok, tok)], v_send.at[i], v_recv.at[i], to))
+
+    def send_q(k, i):
+        other = partner(z, i)
+        pos = (groups - k) % groups * heads + i
+        go(remote(qt.at[hrows(other)], qa.at[pos, pl.ds(0, HD)], q_send.at[pos], q_recv.at[pos],
+                  (lax.rem(r + k, groups) * heads + other, j)))
+
+    for k in range(1, groups):
+        for i in range(heads):
+            send_q(k, i)
+    for i in range(1, heads):
+        send_q(0, i)
+
+    def wrow(owner):
+        return wfull.at[pl.ds(pl.multiple_of(owner * wrows, wrows), wrows)]
+
+    sib = side * 2 + 1 - core
+    go(remote(w_ref, wrow(j), ws_send.at[0], w_recv.at[j], (b, sib)))
+    for k in range(1, nh // 2):
+        to = lax.rem(side + k, nh // 2) * 2 + core
+        go(remote(w_ref, wrow(j), wx_send.at[k], w_recv.at[j], (b, to)))
+
+    lane = lax.broadcasted_iota(jnp.int32, (16, LANES), 1)
+    low_f = (lane < HD).astype(F32)
+    low = low_f.astype(BF16)[:1]
+
+    def onehot(image):
+        return jnp.where(lane == HD + image, 1.0, 0.0).astype(BF16)[:1]
+
+    srow = lax.broadcasted_iota(jnp.int32, (QROWS - HD, BS), 0)
+    for pos in range(n):
+        first = (lax.rem(r + pos // heads, groups) * heads + partner(z, pos % heads)) * per
+        for p in range(per):
+            mask = jnp.where(srow == img_ref[first + p], 0.0, NEG).astype(BF16)
+            qa[pos, pl.ds(HD, QROWS - HD), pl.ds(p * BS, BS)] = mask
+    qa[0, pl.ds(0, HD), :] = qt[hrows(z), :]
+    va[pl.ds(0, HD), pl.ds(0, tok)] = vt[hrows(z), :]
+    va[pl.ds(HD, VROWS - HD), :] = jnp.ones((VROWS - HD, allk), BF16)
+
+    local[3].wait()
+    local[4].wait()
+    traw[...] = jnp.zeros_like(traw)
+    for h in range(heads):
+        c = slice(h * HD, (h + 1) * HD)
+
+        @pl.when(z == h)
+        def _():
+            traw[pl.ds(0, texts), :] = jnp.concatenate([tkin[:, c], tvin[:, c]], axis=1).astype(F32)
+
+    span = -(-tpad // LANES) * LANES
+    raw = traw[pl.ds(r * share, span), :]
+    trow = lax.broadcasted_iota(jnp.int32, raw.shape, 0)
+    tlane = lax.broadcasted_iota(jnp.int32, raw.shape, 1)
+    timg = jnp.zeros_like(trow)
+    for i in range(1, images + 1):
+        timg += (trow + r * share >= i * TEXT).astype(jnp.int32)
+    timg = jnp.where(trow < share, timg, images)
+    taug = jnp.where(tlane < HD, raw, jnp.where(tlane == HD + timg, 1.0, 0.0)).astype(BF16)
+    kaug[pl.ds(keys, tpad), :] = taug[:tpad]
+    va[pl.ds(0, HD), pl.ds(keys, tpad)] = jnp.transpose(raw)[HD:, :tpad].astype(BF16)
+
+    def load_k(i):
+        first = (r * heads + partner(z, i)) * per
+        for p in range(per):
+            at = (p * BS) % half
+            x = ks[z, pl.ds(at, BS), :] if i == 0 else kr[i, pl.ds(at, BS), :]
+            if p * BS >= half:
+                x = pltpu.roll(x.astype(F32), HD, 1).astype(BF16)
+            kaug[pl.ds(i * tok + p * BS, BS), :] = x * low + onehot(img_ref[first + p])
+
+    load_k(0)
+    for i in range(1, heads):
+        remote(ks.at[0], kr.at[i], k_send.at[i], k_recv.at[i], (b, sib)).wait_recv()
+        load_k(i)
+    for i in range(1, heads):
+        remote(vt.at[pl.ds(0, HD)], va.at[pl.ds(0, HD), pl.ds(i * tok, tok)], v_send.at[i], v_recv.at[i],
+               (b, sib)).wait_recv()
+
+    order = [0] + list(range(heads, n)) + list(range(1, heads))
+
+    def arrive(pos):
+        if pos:
+            remote(qt.at[pl.ds(0, HD)], qa.at[pos, pl.ds(0, HD)], q_send.at[pos], q_recv.at[pos],
+                   (b, sib)).wait_recv()
+
+    def scores(pos, slot):
+        s = jnp.dot(kaug[...], qa[pos], preferred_element_type=F32)
+        sb[slot] = s
+        mb[slot] = jnp.broadcast_to(jnp.max(s, axis=0, keepdims=True), mb.shape[1:])
+
+    def attend(pos, slot):
+        top = mb[slot][:1]
+        p = jnp.exp(sb[slot] - top).astype(BF16)
+        o = jnp.dot(va[...], p, preferred_element_type=F32)
+        den = o[HD:HD + 1]
+        y = (o[:HD] / den).astype(BF16)
+        level = top + jnp.log(den)
+        for d in range(nh):
+            osend[pos * nh + d] = y[:, d * td:(d + 1) * td]
+            lsend[pos * nh + d] = level[:, d * td:(d + 1) * td]
+
+    mine = (j * heads + z) * groups + r
+
+    def give(pos, k):
+        dest = lax.rem(j + k, nh)
+        to = (lax.rem(r + pos // heads, groups) * heads + partner(z, pos % heads), dest)
+        if pos == 0 and k == 0:
+            orecv[mine] = osend[dest]
+            lrecv[mine] = lsend[dest]
+        else:
+            at = pos * nh + dest
+            go(remote(osend.at[at], orecv.at[mine], o_send.at[pos * nh + k], o_recv.at[mine], to))
+            go(remote(lsend.at[at], lrecv.at[mine], e_send.at[pos * nh + k], e_recv.at[mine], to))
+
+    def relay_w():
+        for k in range(1, nh // 2):
+            owner = lax.rem(side + nh // 2 - k, nh // 2) * 2 + core
+            remote(w_ref, wrow(owner), ws_send.at[k], w_recv.at[owner], (b, sib)).wait_recv()
+            go(remote(wrow(owner), wrow(owner), ws_send.at[k], w_recv.at[owner], (b, sib)))
+
+    arrive(order[0])
+    scores(order[0], 0)
+    for t in range(n):
+        pos = order[t]
+        if t + 1 < n:
+            arrive(order[t + 1])
+            scores(order[t + 1], (t + 1) % 2)
+        attend(pos, t % 2)
+        for k in range(nh):
+            give(pos, k)
+    relay_w()
+
+    local[5].wait()
+    local[6].wait()
+    for k in range(groups):
+        for i in range(heads):
+            for d in range(nh):
+                if i or k or d:
+                    slot = (lax.rem(j + d, nh) * heads + partner(z, i)) * groups + lax.rem(r + k, groups)
+                    remote(osend.at[0], orecv.at[slot], o_send.at[0], o_recv.at[slot], (b, sib)).wait_recv()
+                    remote(lsend.at[0], lrecv.at[slot], e_send.at[0], e_recv.at[slot], (b, sib)).wait_recv()
+    for h in range(heads * nh):
+        levels = [lrecv[h * groups + g] for g in range(groups)]
+        top = functools.reduce(jnp.maximum, levels)
+        ws = [jnp.exp(x - top) for x in levels]
+        total = functools.reduce(jnp.add, ws)
+        parts = [orecv[h * groups + g].astype(F32) * (ws[g] / total) for g in range(groups)]
+        mixed[pl.ds(h * HD, HD), :] = functools.reduce(jnp.add, parts).astype(BF16)
+    for k in range(nh // 2):
+        owner = lax.rem(side + nh // 2 - k, nh // 2) * 2 + 1 - core
+        remote(w_ref, wrow(owner), ws_send.at[k], w_recv.at[owner], (b, sib)).wait_recv()
+
+    attended = jnp.transpose(mixed[...])
+    unit = min(td, BS)
+    width = 256
+    for t in range(out_ref.shape[1] // width):
+        c = pl.ds(t * width, width)
+        y = jnp.dot(attended, wfull[:, c], preferred_element_type=F32)
+        for u in range(td // unit):
+            image = img_ref[(b * tok + j * td + u * unit) // BS]
+            gate = jnp.zeros((1, width), F32)
+            for m in range(images):
+                gate = jnp.where(image == m, gate_ref[pl.ds(m, 1), c], gate)
+            rows = pl.ds(u * unit, unit)
+            part = y[u * unit:(u + 1) * unit]
+            out_ref[rows, c] = (resv[rows, c].astype(F32) + gate * part).astype(BF16)
+
+    for copy in sent:
+        copy.wait_send()
+
+
+def split_call(n, nh, *args):
+    q, k, v, tk, tv, block_image, gate, res, w = args
+    tok, cols = q.shape
+    heads = cols // HD
+    groups = n // heads
+    td = res.shape[0]
+    share = -(-tk.shape[0] // groups)
+    tpad = -(-share // 16) * 16
+    span = -(-tpad // LANES) * LANES
+    keys = heads * tok + tpad
+    vm = pl.BlockSpec(memory_space=pltpu.VMEM)
+    anyw = pl.BlockSpec(memory_space=pl.ANY)
+    dma = pltpu.SemaphoreType.DMA
+    return pl.pallas_call(
+        functools.partial(split_kernel, n, nh),
+        out_shape=jax.ShapeDtypeStruct(res.shape, BF16),
+        in_specs=[anyw] * 5 + [pl.BlockSpec(memory_space=pltpu.SMEM), vm, anyw, anyw],
+        out_specs=vm,
+        scratch_shapes=[
+            pltpu.VMEM(q.shape, BF16), pltpu.VMEM(k.shape, BF16), pltpu.VMEM(v.shape, BF16),
+            pltpu.VMEM(tk.shape, BF16), pltpu.VMEM(tv.shape, BF16),
+            pltpu.VMEM((cols, tok), BF16), pltpu.VMEM((cols, tok), BF16),
+            pltpu.VMEM((heads, tok // 2, LANES), BF16), pltpu.VMEM((heads, tok // 2, LANES), BF16),
+            pltpu.VMEM((n, QROWS, tok), BF16),
+            pltpu.VMEM((keys, LANES), BF16),
+            pltpu.VMEM((VROWS, keys), BF16),
+            pltpu.VMEM(((groups - 1) * share + max(span, tk.shape[0]) + 8, LANES), F32),
+            pltpu.VMEM((2, keys, tok), F32),
+            pltpu.VMEM((2, 8, tok), F32),
+            pltpu.VMEM((n * nh, HD, td), BF16),
+            pltpu.VMEM((n * nh, 1, td), F32),
+            pltpu.VMEM((n * nh, HD, td), BF16),
+            pltpu.VMEM((n * nh, 1, td), F32),
+            pltpu.VMEM((heads * nh * HD, td), BF16),
+            pltpu.VMEM((w.shape[0] * nh, w.shape[1]), BF16),
+            pltpu.VMEM(res.shape, BF16),
+            dma((n,)), dma((n,)), dma((heads,)), dma((heads,)), dma((heads,)), dma((heads,)),
+            dma((nh,)), dma((nh,)), dma((nh,)),
+            dma((n * nh,)), dma((n * nh,)), dma((n * nh,)), dma((n * nh,)), dma((7,)),
+        ],
+        compiler_params=pltpu.CompilerParams(
+            collective_id=0, has_side_effects=True, vmem_limit_bytes=60 * 1024 * 1024
+        ),
+    )(*args)
+
+
 def solution(mesh):
     n, nh = mesh.shape["blk"], mesh.shape["head"]
 
@@ -269,6 +566,8 @@
         groups = n // heads
         td = res.shape[0]
         rows = heads * tok
+        if groups > 1 and groups <= 4 and td % LANES == 0 and tok % (2 * BS) == 0:
+            return split_call(n, nh, q, k, v, tk, tv, block_image, gate, res, w)
         upad = -(-tk.shape[0] // LANES) * LANES
         vm = pl.BlockSpec(memory_space=pltpu.VMEM)
         anyw = pl.BlockSpec(memory_space=pl.ANY)

time: 41.8 us -> 38.8 us (0.928)
  Pallas kernels: 39.9 us -> 36.8 us
    pallas_call x1, Pallas kernels: 39.9 us -> 36.8 us  [split_call(): pl.pallas_call(functools.partial(split_kernel, n, nh), out_shape=jax.Shap...]
where the time goes in v1:
time: 38.8 us; the launch traced here: 38.6 us
  Pallas kernels  36.8 us (95%)
  local copies, waits for them, and re-layouts  1.77 us (5%)
    pallas_call x1, Pallas kernels, split_call(): pl.pallas_call(functools.partial(split_kernel, n, nh), out_shape=jax.Shap...  36.8 us
    unnamed x1, local copies, waits for them, and re-layouts  1.77 us

profile of v1, /device:TPU:0, one launch (start us, length us, event | category | flops | bytes accessed | tf_op | source)
XLA Modules:
  0.0 38.6 jit_solution(17248442518511294818)
XLA Ops:
  0.0 36.8 %shard_map.91 = bf16[128,1536]{1,0:T(8,128)(2,1)} custom-call(bf16[512,256]{1,0:T(8,128)(2,1)} %q_ref.1, bf16[512,256]{1,0:T(8,128)(2,1)} %k_ref.1, bf16[512,256]{1,0:T(8,128)(2,1)} %v_ref.1, bf16[308,256]{1,0:T(8,128)(2,1)} %tk_ref.1, bf16[308,256]{1,0:T(8,128)(2,1)} %tv_ref.1, s32[32]{0:T(128)} %img_ref.1, f32[2,1536]{1,0:T(2,128)} %gate_ref.1, ...), custom_call_target="tpu_custom_call" | custom-call | tf_op jit(solution)/shard_map/pallas_call | solution.py:527
  36.8 1.8 %copy.11 = bf16[128,1536]{1,0:T(8,128)(2,1)} copy(bf16[128,1536]{1,0:T(8,128)(2,1)} %shard_map.91) | data formatting | bytes 786432

commit v2 on v1

--- a/solution.py
+++ b/solution.py
@@ -265,8 +265,8 @@
 
 
 def split_kernel(
-    n, nh, q_ref, k_ref, v_ref, tk_ref, tv_ref, img_ref, gate_ref, res_ref, w_ref, out_ref,
-    qin, kin, vin, tkin, tvin, qt, vt, ks, kr, qa, kaug, va, traw, sb, mb, osend, lsend, orecv, lrecv,
+    n, nh, q_ref, k_ref, v_ref, tk_ref, tv_ref, img_in, gate_in, res_ref, w_ref, out_ref,
+    qin, kin, vin, tkin, tvin, img_ref, gate_ref, qt, vt, ks, kr, qa, kaug, va, traw, sb, mb, osend, lsend, orecv, lrecv,
     mixed, wfull, resv,
     q_send, q_recv, k_send, k_recv, v_send, v_recv, wx_send, ws_send, w_recv, o_send, o_recv, e_send, e_recv, l_sem,
 ):
@@ -303,6 +303,7 @@
     local = []
     for s, (src, dst) in enumerate(
         ((v_ref, vin), (q_ref, qin), (k_ref, kin), (tk_ref, tkin), (tv_ref, tvin),
+         (img_in, img_ref), (gate_in, gate_ref),
          (w_ref, wfull.at[pl.ds(pl.multiple_of(j * wrows, wrows), wrows)]), (res_ref, resv))
     ):
         copy = pltpu.make_async_copy(src, dst, l_sem.at[s])
@@ -314,11 +315,8 @@
             src_ref=src, dst_ref=dst, send_sem=ss, recv_sem=rs, device_id=to, device_id_type=MESH
         )
 
-    sent = []
-
     def go(copy):
         copy.start()
-        sent.append(copy)
 
     local[0].wait()
     vt[...] = jnp.transpose(vin[...])
@@ -335,32 +333,65 @@
     def hrows(h):
         return pl.ds(pl.multiple_of(h * HD, HD), HD)
 
-    for i in range(1, heads):
+    def send_k(i):
         other = partner(z, i)
-        to = (r * heads + other, j)
-        go(remote(ks.at[other], kr.at[i], k_send.at[i], k_recv.at[i], to))
-        go(remote(vt.at[hrows(other)], va.at[pl.ds(0, HD), pl.ds(i * tok, tok)], v_send.at[i], v_recv.at[i], to))
+        go(remote(ks.at[other], kr.at[i], k_send, k_recv.at[i], (r * heads + other, j)))
+
+    def send_v(i):
+        other = partner(z, i)
+        go(remote(vt.at[hrows(other)], va.at[pl.ds(0, HD), pl.ds(i * tok, tok)], v_send, v_recv,
+                  (r * heads + other, j)))
+
+    flip = (z * 2 // heads + r) % 2 * (heads // 2)
+    near = lax.rem(z + flip, heads)
 
     def send_q(k, i):
-        other = partner(z, i)
-        pos = (groups - k) % groups * heads + i
-        go(remote(qt.at[hrows(other)], qa.at[pos, pl.ds(0, HD)], q_send.at[pos], q_recv.at[pos],
+        at = partner(flip, i) if k else i
+        other = partner(near, i) if k else partner(z, i)
+        pos = (groups - k) % groups * heads + at
+        go(remote(qt.at[hrows(other)], qa.at[pos, pl.ds(0, HD)], q_send, q_recv.at[pos],
                   (lax.rem(r + k, groups) * heads + other, j)))
 
-    for k in range(1, groups):
-        for i in range(heads):
-            send_q(k, i)
-    for i in range(1, heads):
-        send_q(0, i)
+    close = (z * 2 // heads + r) % 2
+
+    def send_cross(part):
+        for k in range(1, groups):
+            for i in part:
+                send_q(k, i)
+
+    def send_within(part):
+        for i in part:
+            send_q(0, i)
 
     def wrow(owner):
         return wfull.at[pl.ds(pl.multiple_of(owner * wrows, wrows), wrows)]
 
     sib = side * 2 + 1 - core
-    go(remote(w_ref, wrow(j), ws_send.at[0], w_recv.at[j], (b, sib)))
-    for k in range(1, nh // 2):
-        to = lax.rem(side + k, nh // 2) * 2 + core
-        go(remote(w_ref, wrow(j), wx_send.at[k], w_recv.at[j], (b, to)))
+    go(remote(w_ref, wrow(j), ws_send, w_recv.at[j], (b, sib)))
+
+    def arrived_w(owner):
+        remote(w_ref, wrow(owner), ws_send, w_recv.at[owner], (b, sib)).wait_recv()
+
+    def cross_w(src, owner):
+        for k in range(1, nh // 2):
+            to = lax.rem(side + k, nh // 2) * 2 + core
+            go(remote(src, wrow(owner), wx_send, w_recv.at[owner], (b, to)))
+
+    partners = list(range(heads // 2, heads)) + list(range(1, heads // 2))
+    for i in partners:
+        send_k(i)
+    for i in partners:
+        send_v(i)
+    send_cross(range(heads // 2))
+    send_within(range(1, heads // 2))
+
+    @pl.when(close == 1)
+    def _():
+        send_within(range(heads // 2, heads))
+
+    @pl.when(core == 1)
+    def _():
+        cross_w(w_ref, j)
 
     lane = lax.broadcasted_iota(jnp.int32, (16, LANES), 1)
     low_f = (lane < HD).astype(F32)
@@ -369,6 +400,7 @@
     def onehot(image):
         return jnp.where(lane == HD + image, 1.0, 0.0).astype(BF16)[:1]
 
+    local[5].wait()
     srow = lax.broadcasted_iota(jnp.int32, (QROWS - HD, BS), 0)
     for pos in range(n):
         first = (lax.rem(r + pos // heads, groups) * heads + partner(z, pos % heads)) * per
@@ -411,76 +443,95 @@
             kaug[pl.ds(i * tok + p * BS, BS), :] = x * low + onehot(img_ref[first + p])
 
     load_k(0)
-    for i in range(1, heads):
-        remote(ks.at[0], kr.at[i], k_send.at[i], k_recv.at[i], (b, sib)).wait_recv()
+    for i in partners:
+        remote(ks.at[0], kr.at[i], k_send, k_recv.at[i], (b, sib)).wait_recv()
         load_k(i)
-    for i in range(1, heads):
-        remote(vt.at[pl.ds(0, HD)], va.at[pl.ds(0, HD), pl.ds(i * tok, tok)], v_send.at[i], v_recv.at[i],
-               (b, sib)).wait_recv()
-
-    order = [0] + list(range(heads, n)) + list(range(1, heads))
+    send_cross(range(heads // 2, heads))
+
+    @pl.when(close == 0)
+    def _():
+        send_within(range(heads // 2, heads))
+
+    def blk(d, place):
+        return lax.rem(r + d, groups) * heads + place
+
+    own = [(i, blk(0, partner(z, i))) for i in range(heads)]
+    cross = [
+        (d * heads + partner(flip, i), blk(d, partner(near, i)))
+        for d in range(1, groups) for i in range(heads)
+    ]
+    order = own[:1] + [
+        tuple(close * u + (1 - close) * v for u, v in zip(one, two))
+        for one, two in zip(cross + own[1:], own[1:] + cross[len(cross) // 2:] + cross[:len(cross) // 2])
+    ]
 
     def arrive(pos):
-        if pos:
-            remote(qt.at[pl.ds(0, HD)], qa.at[pos, pl.ds(0, HD)], q_send.at[pos], q_recv.at[pos],
-                   (b, sib)).wait_recv()
-
-    def scores(pos, slot):
-        s = jnp.dot(kaug[...], qa[pos], preferred_element_type=F32)
-        sb[slot] = s
-        mb[slot] = jnp.broadcast_to(jnp.max(s, axis=0, keepdims=True), mb.shape[1:])
-
-    def attend(pos, slot):
-        top = mb[slot][:1]
-        p = jnp.exp(sb[slot] - top).astype(BF16)
+        remote(qt.at[pl.ds(0, HD)], qa.at[pos, pl.ds(0, HD)], q_send, q_recv.at[pos], (b, sib)).wait_recv()
+
+    def scores(pos, slot, low, width):
+        c = pl.ds(low, width)
+        s = jnp.dot(kaug[...], qa[pos, :, c], preferred_element_type=F32)
+        sb[slot, :, c] = s
+        mb[slot, :, c] = jnp.broadcast_to(jnp.max(s, axis=0, keepdims=True), (mb.shape[1], width))
+
+    def attend(pos, slot, low, width):
+        c = pl.ds(low, width)
+        top = mb[slot, pl.ds(0, 1), c]
+        p = jnp.exp(sb[slot, :, c] - top).astype(BF16)
         o = jnp.dot(va[...], p, preferred_element_type=F32)
         den = o[HD:HD + 1]
         y = (o[:HD] / den).astype(BF16)
         level = top + jnp.log(den)
-        for d in range(nh):
-            osend[pos * nh + d] = y[:, d * td:(d + 1) * td]
-            lsend[pos * nh + d] = level[:, d * td:(d + 1) * td]
+        for d in range(width // td):
+            osend[pos * nh + low // td + d] = y[:, d * td:(d + 1) * td]
+            lsend[pos * nh + low // td + d] = level[:, d * td:(d + 1) * td]
 
     mine = (j * heads + z) * groups + r
 
-    def give(pos, k):
-        dest = lax.rem(j + k, nh)
-        to = (lax.rem(r + pos // heads, groups) * heads + partner(z, pos % heads), dest)
-        if pos == 0 and k == 0:
-            orecv[mine] = osend[dest]
-            lrecv[mine] = lsend[dest]
-        else:
+    def give(pos, owner, dests):
+        for dest in dests:
             at = pos * nh + dest
-            go(remote(osend.at[at], orecv.at[mine], o_send.at[pos * nh + k], o_recv.at[mine], to))
-            go(remote(lsend.at[at], lrecv.at[mine], e_send.at[pos * nh + k], e_recv.at[mine], to))
+            go(remote(osend.at[at], orecv.at[mine], o_send, o_recv, (owner, dest)))
+            go(remote(lsend.at[at], lrecv.at[mine], e_send, e_recv, (owner, dest)))
 
     def relay_w():
-        for k in range(1, nh // 2):
-            owner = lax.rem(side + nh // 2 - k, nh // 2) * 2 + core
-            remote(w_ref, wrow(owner), ws_send.at[k], w_recv.at[owner], (b, sib)).wait_recv()
-            go(remote(wrow(owner), wrow(owner), ws_send.at[k], w_recv.at[owner], (b, sib)))
-
-    arrive(order[0])
-    scores(order[0], 0)
-    for t in range(n):
-        pos = order[t]
+        @pl.when(core == 1)
+        def _():
+            for k in range(1, nh // 2):
+                for c in range(2):
+                    owner = lax.rem(side + k, nh // 2) * 2 + 1 - c
+                    arrived_w(owner)
+                    go(remote(wrow(owner), wrow(owner), ws_send, w_recv.at[owner], (b, sib)))
+
+    scores(0, 0, 0, tok)
+    rest = va.at[pl.ds(0, HD), pl.ds(tok, keys - tok)]
+    remote(rest, rest, v_send, v_recv, (b, sib)).wait_recv()
+    @pl.when(core == 1)
+    def _():
+        arrived_w(sib)
+        cross_w(wrow(sib), sib)
+
+
+    for t, (pos, owner) in enumerate(order):
         if t + 1 < n:
-            arrive(order[t + 1])
-            scores(order[t + 1], (t + 1) % 2)
-        attend(pos, t % 2)
-        for k in range(nh):
-            give(pos, k)
+            arrive(order[t + 1][0])
+            scores(order[t + 1][0], (t + 1) % 2, 0, tok)
+        attend(pos, t % 2, 0, tok)
+        if t == 0:
+            orecv[mine] = osend[j]
+            lrecv[mine] = lsend[j]
+        turns = [(k + nh // 2) % nh for k in range(nh)]
+        give(pos, owner, [lax.rem(j + k, nh) for k in turns if k or t])
     relay_w()
 
-    local[5].wait()
     local[6].wait()
-    for k in range(groups):
-        for i in range(heads):
-            for d in range(nh):
-                if i or k or d:
-                    slot = (lax.rem(j + d, nh) * heads + partner(z, i)) * groups + lax.rem(r + k, groups)
-                    remote(osend.at[0], orecv.at[slot], o_send.at[0], o_recv.at[slot], (b, sib)).wait_recv()
-                    remote(lsend.at[0], lrecv.at[slot], e_send.at[0], e_recv.at[slot], (b, sib)).wait_recv()
+    local[7].wait()
+    local[8].wait()
+    most = pl.ds(0, n * nh - 1)
+    outs = remote(osend.at[most], orecv.at[most], o_send, o_recv, (b, sib))
+    ends = remote(lsend.at[most], lrecv.at[most], e_send, e_recv, (b, sib))
+    outs.wait_recv()
+    ends.wait_recv()
     for h in range(heads * nh):
         levels = [lrecv[h * groups + g] for g in range(groups)]
         top = functools.reduce(jnp.maximum, levels)
@@ -488,9 +539,12 @@
         total = functools.reduce(jnp.add, ws)
         parts = [orecv[h * groups + g].astype(F32) * (ws[g] / total) for g in range(groups)]
         mixed[pl.ds(h * HD, HD), :] = functools.reduce(jnp.add, parts).astype(BF16)
-    for k in range(nh // 2):
-        owner = lax.rem(side + nh // 2 - k, nh // 2) * 2 + 1 - core
-        remote(w_ref, wrow(owner), ws_send.at[k], w_recv.at[owner], (b, sib)).wait_recv()
+    @pl.when(core == 0)
+    def _():
+        arrived_w(sib)
+        for k in range(1, nh // 2):
+            for c in range(2):
+                arrived_w(lax.rem(side + k, nh // 2) * 2 + c)
 
     attended = jnp.transpose(mixed[...])
     unit = min(td, BS)
@@ -507,8 +561,21 @@
             part = y[u * unit:(u + 1) * unit]
             out_ref[rows, c] = (resv[rows, c].astype(F32) + gate * part).astype(BF16)
 
-    for copy in sent:
-        copy.wait_send()
+    outs.wait_send()
+    ends.wait_send()
+    most = pl.ds(0, heads - 1)
+    remote(ks.at[most], kr.at[most], k_send, k_recv.at[0], (b, sib)).wait_send()
+    remote(rest, rest, v_send, v_recv, (b, sib)).wait_send()
+    most = pl.ds(0, n - 1)
+    part = qa.at[most, pl.ds(0, HD)]
+    remote(part, part, q_send, q_recv.at[0], (b, sib)).wait_send()
+    remote(w_ref, wrow(j), ws_send, w_recv.at[j], (b, sib)).wait_send()
+
+    @pl.when(core == 1)
+    def _():
+        part = wfull.at[pl.ds(0, (nh - 2) * wrows)]
+        remote(part, part, wx_send, w_recv.at[0], (b, sib)).wait_send()
+        remote(part, part, ws_send, w_recv.at[0], (b, sib)).wait_send()
 
 
 def split_call(n, nh, *args):
@@ -522,16 +589,17 @@
     span = -(-tpad // LANES) * LANES
     keys = heads * tok + tpad
     vm = pl.BlockSpec(memory_space=pltpu.VMEM)
-    anyw = pl.BlockSpec(memory_space=pl.ANY)
+    hbm = pl.BlockSpec(memory_space=pltpu.HBM)
     dma = pltpu.SemaphoreType.DMA
     return pl.pallas_call(
         functools.partial(split_kernel, n, nh),
-        out_shape=jax.ShapeDtypeStruct(res.shape, BF16),
-        in_specs=[anyw] * 5 + [pl.BlockSpec(memory_space=pltpu.SMEM), vm, anyw, anyw],
+        out_shape=pltpu.VMEM(res.shape, BF16),
+        in_specs=[hbm] * 9,
         out_specs=vm,
         scratch_shapes=[
             pltpu.VMEM(q.shape, BF16), pltpu.VMEM(k.shape, BF16), pltpu.VMEM(v.shape, BF16),
             pltpu.VMEM(tk.shape, BF16), pltpu.VMEM(tv.shape, BF16),
+            pltpu.SMEM(block_image.shape, jnp.int32), pltpu.VMEM(gate.shape, F32),
             pltpu.VMEM((cols, tok), BF16), pltpu.VMEM((cols, tok), BF16),
             pltpu.VMEM((heads, tok // 2, LANES), BF16), pltpu.VMEM((heads, tok // 2, LANES), BF16),
             pltpu.VMEM((n, QROWS, tok), BF16),
@@ -547,14 +615,13 @@
             pltpu.VMEM((heads * nh * HD, td), BF16),
             pltpu.VMEM((w.shape[0] * nh, w.shape[1]), BF16),
             pltpu.VMEM(res.shape, BF16),
-            dma((n,)), dma((n,)), dma((heads,)), dma((heads,)), dma((heads,)), dma((heads,)),
-            dma((nh,)), dma((nh,)), dma((nh,)),
-            dma((n * nh,)), dma((n * nh,)), dma((n * nh,)), dma((n * nh,)), dma((7,)),
+            dma, dma((n,)), dma, dma((heads,)), dma, dma,
+            dma, dma, dma((nh,)), dma, dma, dma, dma, dma((9,)),
         ],
         compiler_params=pltpu.CompilerParams(
-            collective_id=0, has_side_effects=True, vmem_limit_bytes=60 * 1024 * 1024
+            collective_id=0, has_side_effects=True, vmem_limit_bytes=40 * 1024 * 1024
         ),
-    )(*args)
+    )(*(pltpu.with_memory_space_constraint(x, pltpu.HBM) for x in args))
 
 
 def solution(mesh):
@@ -566,7 +633,7 @@
         groups = n // heads
         td = res.shape[0]
         rows = heads * tok
-        if groups > 1 and groups <= 4 and td % LANES == 0 and tok % (2 * BS) == 0:
+        if 1 < groups <= 4 and heads > 1 and td % LANES == 0 and tok % (2 * BS) == 0:
             return split_call(n, nh, q, k, v, tk, tv, block_image, gate, res, w)
         upad = -(-tk.shape[0] // LANES) * LANES
         vm = pl.BlockSpec(memory_space=pltpu.VMEM)

time: 38.8 us -> 34.9 us (0.90)
  Pallas kernels: 36.8 us -> 34 us
  local copies, waits for them, and re-layouts: 1.77 us -> 0.75 us
    pallas_call x1, Pallas kernels: 36.8 us -> 34 us  [split_call(): pl.pallas_call(functools.partial(split_kernel, n, nh), out_shape=pltpu.VM...]
    unnamed x1, local copies, waits for them, and re-layouts: 1.77 us -> 0.75 us
where the time goes in v2:
time: 34.9 us; the launch traced here: 34.8 us
  Pallas kernels  34 us (97%)
  local copies, waits for them, and re-layouts  0.75 us (2%)
    pallas_call x1, Pallas kernels, split_call(): pl.pallas_call(functools.partial(split_kernel, n, nh), out_shape=pltpu.VM...  34 us
    unnamed x1, local copies, waits for them, and re-layouts  0.75 us

profile of v2, /device:TPU:0, one launch (start us, length us, event | category | flops | bytes accessed | tf_op | source)
XLA Modules:
  0.0 34.8 jit_solution(1788110859896117906)
XLA Ops:
  0.0 34.0 %shard_map.91 = bf16[128,1536]{1,0:T(8,128)(2,1)S(1)} custom-call(bf16[512,256]{1,0:T(8,128)(2,1)} %q_ref.1, bf16[512,256]{1,0:T(8,128)(2,1)} %k_ref.1, bf16[512,256]{1,0:T(8,128)(2,1)} %v_ref.1, bf16[308,256]{1,0:T(8,128)(2,1)} %tk_ref.1, bf16[308,256]{1,0:T(8,128)(2,1)} %tv_ref.1, s32[32]{0:T(128)} %img_in.1, f32[2,1536]{1,0:T(2,128)} %gate_in.1, ...), custom_call_target="tpu_custom_call" | custom-call | tf_op jit(solution)/shard_map/pallas_call | solution.py:594
  34.0 0.7 %copy.11 = bf16[128,1536]{1,0:T(8,128)(2,1)} copy(bf16[128,1536]{1,0:T(8,128)(2,1)S(1)} %shard_map.91) | data formatting | bytes 786432

commit v3 on v2

--- a/solution.py
+++ b/solution.py
@@ -268,7 +268,7 @@
     n, nh, q_ref, k_ref, v_ref, tk_ref, tv_ref, img_in, gate_in, res_ref, w_ref, out_ref,
     qin, kin, vin, tkin, tvin, img_ref, gate_ref, qt, vt, ks, kr, qa, kaug, va, traw, sb, mb, osend, lsend, orecv, lrecv,
     mixed, wfull, resv,
-    q_send, q_recv, k_send, k_recv, v_send, v_recv, wx_send, ws_send, w_recv, o_send, o_recv, e_send, e_recv, l_sem,
+    q_send, q_recv, k_send, k_recv, v_send, v_recv, wx_send, ws_send, w_recv, o_send, o_recv, e_send, e_recv, l_sem, told,
 ):
     tok, cols = q_ref.shape
     heads = cols // HD
@@ -289,16 +289,19 @@
     side, core = j // 2, j % 2
 
     barrier = pltpu.get_barrier_semaphore()
-    count = 0
-    for k in range(groups):
+    close = (z * 2 // heads + r) % 2
+    for i in range(1, heads):
+        pl.semaphore_signal(barrier, inc=1, device_id=(r * heads + partner(z, i), j), device_id_type=MESH)
+
+    @pl.when(close == 1)
+    def _():
         for i in range(heads):
-            if i or k:
-                to = (lax.rem(r + k, groups) * heads + partner(z, i), j)
-                pl.semaphore_signal(barrier, inc=1, device_id=to, device_id_type=MESH)
-                count += 1
+            to = (lax.rem(r + 1, groups) * heads + partner(z, i), j)
+            pl.semaphore_signal(barrier, inc=1, device_id=to, device_id_type=MESH)
+
+    count = heads - 1 + heads // 2 + nh - 1
     for k in range(1, nh):
         pl.semaphore_signal(barrier, inc=1, device_id=(b, lax.rem(j + k, nh)), device_id_type=MESH)
-        count += 1
 
     local = []
     for s, (src, dst) in enumerate(
@@ -342,7 +345,7 @@
         go(remote(vt.at[hrows(other)], va.at[pl.ds(0, HD), pl.ds(i * tok, tok)], v_send, v_recv,
                   (r * heads + other, j)))
 
-    flip = (z * 2 // heads + r) % 2 * (heads // 2)
+    flip = close * (heads // 2)
     near = lax.rem(z + flip, heads)
 
     def send_q(k, i):
@@ -351,8 +354,6 @@
         pos = (groups - k) % groups * heads + at
         go(remote(qt.at[hrows(other)], qa.at[pos, pl.ds(0, HD)], q_send, q_recv.at[pos],
                   (lax.rem(r + k, groups) * heads + other, j)))
-
-    close = (z * 2 // heads + r) % 2
 
     def send_cross(part):
         for k in range(1, groups):
@@ -442,16 +443,6 @@
                 x = pltpu.roll(x.astype(F32), HD, 1).astype(BF16)
             kaug[pl.ds(i * tok + p * BS, BS), :] = x * low + onehot(img_ref[first + p])
 
-    load_k(0)
-    for i in partners:
-        remote(ks.at[0], kr.at[i], k_send, k_recv.at[i], (b, sib)).wait_recv()
-        load_k(i)
-    send_cross(range(heads // 2, heads))
-
-    @pl.when(close == 0)
-    def _():
-        send_within(range(heads // 2, heads))
-
     def blk(d, place):
         return lax.rem(r + d, groups) * heads + place
 
@@ -460,13 +451,34 @@
         (d * heads + partner(flip, i), blk(d, partner(near, i)))
         for d in range(1, groups) for i in range(heads)
     ]
+    def arrive(pos):
+        remote(qt.at[pl.ds(0, HD)], qa.at[pos, pl.ds(0, HD)], q_send, q_recv.at[pos], (b, sib)).wait_recv()
+
+    load_k(0)
+    for i in partners:
+        remote(ks.at[0], kr.at[i], k_send, k_recv.at[i], (b, sib)).wait_recv()
+        load_k(i)
+
+    @pl.when(close == 1)
+    def _():
+        arrive(cross[0][0])
+        to = (r * heads + partner(z, heads // 2), j)
+        pl.semaphore_signal(told, inc=1, device_id=to, device_id_type=MESH)
+
+    @pl.when(close == 0)
+    def _():
+        pl.semaphore_wait(told, 1)
+
+    send_cross(range(heads // 2, heads))
+
+    @pl.when(close == 0)
+    def _():
+        send_within(range(heads // 2, heads))
+
     order = own[:1] + [
         tuple(close * u + (1 - close) * v for u, v in zip(one, two))
         for one, two in zip(cross + own[1:], own[1:] + cross[len(cross) // 2:] + cross[:len(cross) // 2])
     ]
-
-    def arrive(pos):
-        remote(qt.at[pl.ds(0, HD)], qa.at[pos, pl.ds(0, HD)], q_send, q_recv.at[pos], (b, sib)).wait_recv()
 
     def scores(pos, slot, low, width):
         c = pl.ds(low, width)
@@ -514,7 +526,10 @@
 
     for t, (pos, owner) in enumerate(order):
         if t + 1 < n:
-            arrive(order[t + 1][0])
+            if t:
+                arrive(order[t + 1][0])
+            else:
+                pl.when(close == 0)(lambda: arrive(own[1][0]))
             scores(order[t + 1][0], (t + 1) % 2, 0, tok)
         attend(pos, t % 2, 0, tok)
         if t == 0:
@@ -616,7 +631,7 @@
             pltpu.VMEM((w.shape[0] * nh, w.shape[1]), BF16),
             pltpu.VMEM(res.shape, BF16),
             dma, dma((n,)), dma, dma((heads,)), dma, dma,
-            dma, dma, dma((nh,)), dma, dma, dma, dma, dma((9,)),
+            dma, dma, dma((nh,)), dma, dma, dma, dma, dma((9,)), pltpu.SemaphoreType.REGULAR,
         ],
         compiler_params=pltpu.CompilerParams(
             collective_id=0, has_side_effects=True, vmem_limit_bytes=40 * 1024 * 1024
@@ -633,7 +648,7 @@
         groups = n // heads
         td = res.shape[0]
         rows = heads * tok
-        if 1 < groups <= 4 and heads > 1 and td % LANES == 0 and tok % (2 * BS) == 0:
+        if groups == 2 and heads > 1 and td % LANES == 0 and tok % (2 * BS) == 0:
             return split_call(n, nh, q, k, v, tk, tv, block_image, gate, res, w)
         upad = -(-tk.shape[0] // LANES) * LANES
         vm = pl.BlockSpec(memory_space=pltpu.VMEM)

time: 34.9 us -> 34.1 us (0.977)
  Pallas kernels: 34 us -> 33 us
    pallas_call x1, Pallas kernels: 34 us -> 33 us  [split_call(): pl.pallas_call(functools.partial(split_kernel, n, nh), out_shape=pltpu.VM...]
where the time goes in v3:
time: 34.1 us; the launch traced here: 33.8 us
  Pallas kernels  33 us (97%)
  local copies, waits for them, and re-layouts  0.75 us (2%)
    pallas_call x1, Pallas kernels, split_call(): pl.pallas_call(functools.partial(split_kernel, n, nh), out_shape=pltpu.VM...  33 us
    unnamed x1, local copies, waits for them, and re-layouts  0.75 us

profile of v3, /device:TPU:0, one launch (start us, length us, event | category | flops | bytes accessed | tf_op | source)
XLA Modules:
  0.0 33.8 jit_solution(8361265183298271565)
XLA Ops:
  0.0 33.0 %shard_map.91 = bf16[128,1536]{1,0:T(8,128)(2,1)S(1)} custom-call(bf16[512,256]{1,0:T(8,128)(2,1)} %q_ref.1, bf16[512,256]{1,0:T(8,128)(2,1)} %k_ref.1, bf16[512,256]{1,0:T(8,128)(2,1)} %v_ref.1, bf16[308,256]{1,0:T(8,128)(2,1)} %tk_ref.1, bf16[308,256]{1,0:T(8,128)(2,1)} %tv_ref.1, s32[32]{0:T(128)} %img_in.1, f32[2,1536]{1,0:T(2,128)} %gate_in.1, ...), custom_call_target="tpu_custom_call" | custom-call | tf_op jit(solution)/shard_map/pallas_call | solution.py:609
  33.1 0.7 %copy.11 = bf16[128,1536]{1,0:T(8,128)(2,1)} copy(bf16[128,1536]{1,0:T(8,128)(2,1)S(1)} %shard_map.91) | data formatting | bytes 786432

commit v4 on v3

--- a/solution.py
+++ b/solution.py
@@ -503,8 +503,8 @@
     def give(pos, owner, dests):
         for dest in dests:
             at = pos * nh + dest
+            go(remote(lsend.at[at], lrecv.at[mine], e_send, e_recv, (owner, dest)))
             go(remote(osend.at[at], orecv.at[mine], o_send, o_recv, (owner, dest)))
-            go(remote(lsend.at[at], lrecv.at[mine], e_send, e_recv, (owner, dest)))
 
     def relay_w():
         @pl.when(core == 1)

time: 34.1 us -> 34.1 us (level)
  no operation moved by 1% of the time
where the time goes in v4:
time: 34.1 us; the launch traced here: 33.8 us
  Pallas kernels  33 us (97%)
  local copies, waits for them, and re-layouts  0.75 us (2%)
    pallas_call x1, Pallas kernels, split_call(): pl.pallas_call(functools.partial(split_kernel, n, nh), out_shape=pltpu.VM...  33 us
    unnamed x1, local copies, waits for them, and re-layouts  0.75 us

profile of v4, /device:TPU:0, one launch (start us, length us, event | category | flops | bytes accessed | tf_op | source)
XLA Modules:
  0.0 33.8 jit_solution(6474786501233379515)
XLA Ops:
  0.0 33.0 %shard_map.91 = bf16[128,1536]{1,0:T(8,128)(2,1)S(1)} custom-call(bf16[512,256]{1,0:T(8,128)(2,1)} %q_ref.1, bf16[512,256]{1,0:T(8,128)(2,1)} %k_ref.1, bf16[512,256]{1,0:T(8,128)(2,1)} %v_ref.1, bf16[308,256]{1,0:T(8,128)(2,1)} %tk_ref.1, bf16[308,256]{1,0:T(8,128)(2,1)} %tv_ref.1, s32[32]{0:T(128)} %img_in.1, f32[2,1536]{1,0:T(2,128)} %gate_in.1, ...), custom_call_target="tpu_custom_call" | custom-call | tf_op jit(solution)/shard_map/pallas_call | solution.py:609
  33.1 0.7 %copy.11 = bf16[128,1536]{1,0:T(8,128)(2,1)} copy(bf16[128,1536]{1,0:T(8,128)(2,1)S(1)} %shard_map.91) | data formatting | bytes 786432
